TPU v7x, 512 devices: a whole 4x4x16 slice. The times are simulated.
512 devices in a mesh: prow: 32 (over z, y_hi), pcol: 16 (over y_lo, x, core).
Axes of the slice: x: 4, y: 4 (y_hi: 2, y_lo: 2; y = y_hi * 2 + y_lo), z: 16, core: 2. Of those that a mesh axis runs over, the one named last changes fastest.
Arguments:
- matrix: float32 [8192, 8192], P('prow', 'pcol'), as said below
Outputs:
- complement: float32 [8192, 8192], P('prow', 'pcol')
- panel_columns: float32 [8192, 512], P(('prow', 'pcol'))
- pivot_values: float32 [512], replicated
Inputs may be any that keep to these rules, and one draw needn't show every extreme that they name: matrix is symmetric and positive definite, with its smallest eigenvalue above a six-hundredth of its largest diagonal entry.
All inputs are finite; a program needn't handle non-finite values.
Results may differ from a plain program's by a relative error of at most 0.00014.
Values sent between devices are 32-bit elements; how exact they have to be, the bound alone decides.
No kernel may reach another device: no remote copies, remote signals or barrier semaphores. Data moves between devices by JAX's collectives and lax.ppermute only.
A program may use at most 128 MiB of HBM per device.

v0:
```python
import jax
import jax.numpy as jnp
from jax import lax
from jax.sharding import Mesh
from jax.sharding import PartitionSpec as P

NB = 256
PANELS = 2
PROW = ("prow_0", "prow_1")
PROW_PCOL = ("prow_0", "prow_1", "pcol")
HIGHEST = lax.Precision.HIGHEST


def from_root(array, axes, root):
    array = jnp.where(lax.axis_index(axes) == root, array, jnp.zeros_like(array))
    for axis in axes:
        array = lax.psum(array, axis)
    return array


def picked(array, axis, root):
    return lax.dynamic_index_in_dim(lax.all_gather(array, axis), root, 0, keepdims=False)


def factor_diagonal(diagonal):
    cholesky_factor = jnp.linalg.cholesky(diagonal)
    scaling = jnp.diagonal(cholesky_factor)
    identity = jnp.eye(diagonal.shape[0], dtype=diagonal.dtype)
    inverse = jax.scipy.linalg.solve_triangular(cholesky_factor, identity, lower=True)
    return (inverse, scaling)


def against(left_side, right_side):
    return lax.dot_general(left_side, right_side, (((1,), (1,)), ((), ())), precision=HIGHEST)


def refreshed(current, weighed, partner, finished, row_base, col_base, bounds):
    row_start, row_stop, col_start, col_stop = bounds
    section = current - against(weighed, partner)
    extent = section.shape
    global_rows = row_base + row_start + lax.broadcasted_iota(jnp.int32, extent, 0)
    global_cols = col_base + col_start + lax.broadcasted_iota(jnp.int32, extent, 1)
    retained = (global_rows >= finished) & (global_cols >= finished)
    return jnp.where(retained, section, jnp.zeros_like(section))


def on_device(matrix):
    current = matrix
    row_count, col_count = matrix.shape
    col_groups = lax.axis_size("pcol")
    row_base = lax.axis_index(PROW) * row_count
    col_base = lax.axis_index("pcol") * col_count
    portion = row_count // col_groups
    column_list = []
    pivot_list = []
    for panel in range(PANELS):
        first = panel * NB
        root_row = first // row_count
        row_offset = first % row_count
        root_col = first // col_count
        col_offset = first % col_count
        row_strip = current
        received = from_root(row_strip, PROW, root_row)
        inverse, scaling = factor_diagonal(received[:, col_offset : col_offset + NB])
        projected = against(current[:, col_offset : col_offset + NB], inverse)
        factored, inverse, scaling = (
            picked(projected * scaling, "pcol", root_col),
            picked(inverse, "pcol", root_col),
            picked(scaling, "pcol", root_col),
        )
        partner = (
            lax.dot_general(received, inverse, (((0,), (1,)), ((), ())), precision=HIGHEST)
            * scaling
        )
        pivot = scaling * scaling
        weighed = factored / pivot
        finished = first + NB
        bounds_list = [(0, row_count, 0, col_count)]
        joined_axis = 1
        sections = [
            refreshed(current, weighed, partner, finished, row_base, col_base, bounds)
            for bounds in bounds_list
        ]
        current = sections[0]
        column_list.append(
            lax.dynamic_slice_in_dim(factored, lax.axis_index("pcol") * portion, portion, 0)
        )
        pivot_list.append(pivot)
    return (current, jnp.concatenate(column_list, axis=1), jnp.concatenate(pivot_list))


def solution(mesh):
    split = Mesh(mesh.devices.reshape(16, 2, mesh.shape["pcol"]), ("prow_0", "prow_1", "pcol"))
    in_specs = (P(PROW, "pcol"),)
    out_specs = (P(PROW, "pcol"), P(PROW_PCOL, None), P())
    return jax.shard_map(
        on_device, mesh=split, in_specs=in_specs, out_specs=out_specs, check_vma=False
    )
```

profile of v0, /device:TPU:1, one launch (start us, length us, event | category | flops | bytes accessed | tf_op | source)
XLA Modules:
  0.0 724.1 jit_solution(15212557457940428483)
XLA Ops:
  7.2 1.2 copy.24
  9.4 134.9 %all-reduce.6.cloned.1.call-done = f32[256,512]{0,1:T(8,128)} async-done(((f32[256,512]{0,1:T(8,128)}), f32[256,512]{0,1:T(8,128)}) %all-reduce.6.cloned.1.call-update) | async-done | bytes 524304 | tf_op jit(solution)/shard_map/psum | solution.py:17
  144.4 61.1 %all-reduce.8.cloned.1.call-done = f32[256,512]{0,1:T(8,128)} async-done(((f32[256,512]{0,1:T(8,128)}), f32[256,512]{0,1:T(8,128)}) %all-reduce.8.cloned.1.call-update) | async-done | bytes 524304 | tf_op jit(solution)/shard_map/psum | solution.py:17
  207.7 11.7 %cholesky.130 = f32[128,128]{1,0:T(8,128)S(1)} custom-call(f32[128,128]{1,0:T(8,128)S(1)} %cholesky.194), custom_call_target="Cholesky" | custom-call | tf_op jit(solution)/shard_map/jit(cholesky)/cholesky | solution.py:26
  219.4 9.8 %custom-call.17 = f32[1,128,128]{1,2,0:T(8,128)S(1)} custom-call(f32[1,128,128]{2,1,0:T(8,128)S(1)} %get-tuple-element.61), custom_call_target="InvertDiagBlocksLowerTriangular" | custom-call | tf_op jit(solution)/shard_map/jit(cholesky)/cholesky | solution.py:26
  229.8 11.7 %cholesky.147 = f32[128,128]{1,0:T(8,128)S(1)} custom-call(f32[128,128]{1,0:T(8,128)S(1)} %convolution_subtract_fusion.5), custom_call_target="Cholesky" | custom-call | tf_op jit(solution)/shard_map/jit(cholesky)/cholesky | solution.py:26
  243.6 4.2 while.4
  244.4 1.4 bitcast_dynamic-update-slice_fusion.4
  246.4 1.4 bitcast_dynamic-update-slice_fusion.4
  247.8 19.7 %custom-call.18 = f32[2,128,128]{1,2,0:T(8,128)S(1)} custom-call(f32[2,128,128]{2,1,0:T(8,128)S(1)} %get-tuple-element.19), custom_call_target="InvertDiagBlocksLowerTriangular" | custom-call | tf_op jit(solution)/shard_map/jit(_solve_triangular)/triangular_solve | solution.py:29
  269.2 2.3 gather_fusion
  272.8 19.3 %all-gather.6 = f32[16,1,256]{2,1,0:T(1,128)S(1)} all-gather(f32[1,1,256]{2,1,0:T(1,128)S(1)} %bitcast.82), channel_id=3, replica_groups=mesh['prow_0'=16,'prow_1'=2,'pcol'=16] {'pcol'}, dimensions={0}, use_global_device_ids=true | all-gather | bytes 17408 | tf_op jit(solution)/shard_map/all_gather | solution.py:22
  292.1 22.0 %all-gather.15.cloned.1.call-done = f32[4096,256]{1,0:T(8,128)} async-done(((f32[256,256]{1,0:T(8,128)}), f32[4096,256]{1,0:T(8,128)}) %all-gather.15.cloned.1.call-update) | async-done | bytes 4194320 | tf_op jit(solution)/shard_map/all_gather | solution.py:22
  314.1 1.6 convolution_multiply_fusion.1
  315.7 45.4 %all-gather.13.cloned.1.call-done = f32[4096,256]{0,1:T(8,128)} async-done(((f32[256,256]{0,1:T(8,128)}), f32[4096,256]{0,1:T(8,128)}) %all-gather.13.cloned.1.call-update) | async-done | bytes 4194320 | tf_op jit(solution)/shard_map/all_gather | solution.py:22
  361.0 2.4 broadcast_select_fusion
  363.5 128.0 %all-reduce.10.cloned.1.call-done = f32[256,512]{0,1:T(8,128)} async-done(((f32[256,512]{0,1:T(8,128)}), f32[256,512]{0,1:T(8,128)}) %all-reduce.10.cloned.1.call-update) | async-done | bytes 524304 | tf_op jit(solution)/shard_map/psum | solution.py:17
  491.6 61.0 %all-reduce.12.cloned.1.call-done = f32[256,512]{0,1:T(8,128)} async-done(((f32[256,512]{0,1:T(8,128)}), f32[256,512]{0,1:T(8,128)}) %all-reduce.12.cloned.1.call-update) | async-done | bytes 524304 | tf_op jit(solution)/shard_map/psum | solution.py:17
  554.8 11.7 %cholesky.164 = f32[128,128]{1,0:T(8,128)S(1)} custom-call(f32[128,128]{1,0:T(8,128)S(1)} %cholesky.197), custom_call_target="Cholesky" | custom-call | tf_op jit(solution)/shard_map/jit(cholesky)/cholesky | solution.py:26
  567.2 9.8 %custom-call.19 = f32[1,128,128]{1,2,0:T(8,128)S(1)} custom-call(f32[1,128,128]{2,1,0:T(8,128)S(1)} %get-tuple-element.57), custom_call_target="InvertDiagBlocksLowerTriangular" | custom-call | tf_op jit(solution)/shard_map/jit(cholesky)/cholesky | solution.py:26
  577.5 11.7 %cholesky.181 = f32[128,128]{1,0:T(8,128)S(1)} custom-call(f32[128,128]{1,0:T(8,128)S(1)} %convolution_subtract_fusion.4), custom_call_target="Cholesky" | custom-call | tf_op jit(solution)/shard_map/jit(cholesky)/cholesky | solution.py:26
  591.3 2.6 gather_fusion.1
  593.9 4.0 while.5
  594.5 1.4 bitcast_dynamic-update-slice_fusion.5
  596.5 1.4 bitcast_dynamic-update-slice_fusion.5
  597.9 19.7 %custom-call.20 = f32[2,128,128]{1,2,0:T(8,128)S(1)} custom-call(f32[2,128,128]{2,1,0:T(8,128)S(1)} %get-tuple-element.20), custom_call_target="InvertDiagBlocksLowerTriangular" | custom-call | tf_op jit(solution)/shard_map/jit(_solve_triangular)/triangular_solve | solution.py:29
  618.5 1.3 convolution_multiply_fusion.2
  620.8 19.3 %all-gather.7 = f32[16,1,256]{2,1,0:T(1,128)S(1)} all-gather(f32[1,1,256]{2,1,0:T(1,128)S(1)} %bitcast.81), channel_id=6, replica_groups=mesh['prow_0'=16,'prow_1'=2,'pcol'=16] {'pcol'}, dimensions={0}, use_global_device_ids=true | all-gather | bytes 17408 | tf_op jit(solution)/shard_map/all_gather | solution.py:22
  640.7 24.0 %all-gather.17.cloned.1.call-done = f32[4096,256]{1,0:T(8,128)} async-done(((f32[256,256]{1,0:T(8,128)}), f32[4096,256]{1,0:T(8,128)}) %all-gather.17.cloned.1.call-update) | async-done | bytes 4194320 | tf_op jit(solution)/shard_map/all_gather | solution.py:22
  665.8 46.7 %all-gather.19.cloned.1.call-done = f32[4096,256]{1,0:T(8,128)} async-done(((f32[256,256]{1,0:T(8,128)}), f32[4096,256]{1,0:T(8,128)}) %all-gather.19.cloned.1.call-update) | async-done | bytes 4194320 | tf_op jit(solution)/shard_map/all_gather | solution.py:22
  712.5 1.6 convolution_multiply_fusion
  714.1 1.6 fusion
  (86 shorter events, 18.9 us)
Async XLA Ops:
  7.2 137.1 %all-reduce.6.cloned.1.call-start = ((), (), s32[]{:S(2)}) async-start(), calls=%async_computation | async-start | bytes 1048576 | tf_op jit(solution)/shard_map/psum | solution.py:17
  9.3 196.2 %all-reduce.8.cloned.1.call-start = ((), (), s32[]{:S(2)}) async-start(), calls=%async_computation.1 | async-start | bytes 1048576 | tf_op jit(solution)/shard_map/psum | solution.py:17
  144.3 127.2 %copy-start.2 = (f32[256,512]{1,0:T(8,128)S(1)}, f32[256,512]{1,0:T(8,128)}, u32[]{:S(2)}) copy-start(f32[256,512]{1,0:T(8,128)} %param.4) | copy-start | bytes 1572868
  144.3 169.8 %all-gather.15.cloned.1.call-start = ((), (), s32[]{:S(2)}) async-start(), calls=%async_computation.5 | async-start | bytes 4456448 | tf_op jit(solution)/shard_map/all_gather | solution.py:22
  206.5 107.6 %copy-start.1 = (f32[256,512]{0,1:T(8,128)S(1)}, f32[256,512]{0,1:T(8,128)}, u32[]{:S(2)}) copy-start(f32[256,512]{0,1:T(8,128)} %all-reduce.8.cloned.1.call-done) | copy-start | bytes 1572868
  269.1 91.9 %all-gather.13.cloned.1.call-start = ((), (), s32[]{:S(2)}) async-start(), calls=%async_computation.4 | async-start | bytes 4456448 | tf_op jit(solution)/shard_map/all_gather | solution.py:22
  272.7 218.9 %all-reduce.10.cloned.1.call-start = ((), (), s32[]{:S(2)}) async-start(), calls=%async_computation.2 | async-start | bytes 1048576 | tf_op jit(solution)/shard_map/psum | solution.py:17
  363.5 189.2 %all-reduce.12.cloned.1.call-start = ((), (), s32[]{:S(2)}) async-start(), calls=%async_computation.3 | async-start | bytes 1048576 | tf_op jit(solution)/shard_map/psum | solution.py:17
  491.6 173.2 %all-gather.17.cloned.1.call-start = ((), (), s32[]{:S(2)}) async-start(), calls=%async_computation.6 | async-start | bytes 4456448 | tf_op jit(solution)/shard_map/all_gather | solution.py:22
  553.8 66.9 %slice-start = ((f32[4096,256]{0,1:T(8,128)}), f32[256,256]{0,1:T(8,128)S(1)}, s32[]{:S(2)}) async-start(f32[4096,256]{0,1:T(8,128)} %all-gather.13.cloned.1.call-done), calls=%async_computation.8 | async-start | bytes 524288 | tf_op jit(solution)/shard_map/jit(dynamic_index_in_dim)/dynamic_slice | solution.py:22
  577.0 135.5 %copy-start = (f32[256,512]{0,1:T(8,128)S(1)}, f32[256,512]{0,1:T(8,128)}, u32[]{:S(2)}) copy-start(f32[256,512]{0,1:T(8,128)} %all-reduce.12.cloned.1.call-done) | copy-start | bytes 1572868
  619.8 92.7 %all-gather.19.cloned.1.call-start = ((), (), s32[]{:S(2)}) async-start(), calls=%async_computation.7 | async-start | bytes 4456448 | tf_op jit(solution)/shard_map/all_gather | solution.py:22
Sparse Core Ops, SparseCore 0:
  10.9 133.3 all-reduce.5
  147.2 58.3 all-reduce.7
  269.2 44.8 all-gather.14
  316.0 44.9 all-gather.12
  363.8 127.7 all-reduce.9
  494.3 58.3 all-reduce.11
  619.9 44.7 all-gather.16
  667.5 44.9 all-gather.18
where the time goes:
time: 725 us; the launch traced here: 724 us
  waiting for transfers between devices  523 us (72%)
  other arithmetic  114 us (16%)
  blocking collectives  38.7 us (5%)
  local copies, waits for them, and re-layouts  18.5 us (3%)
  between operations  17.1 us (2%)
  matrix products  12.3 us (2%)
    psum x4, waiting for transfers between devices, from_root(): array = lax.psum(array, axis)  385 us
    all_gather x4, waiting for transfers between devices, picked(): lax.all_gather(array, axis)  138 us
    another operation x13, other arithmetic, factor_diagonal(): cholesky_factor = jnp.linalg.cholesky(diagonal)  68.5 us
    another operation x7, other arithmetic, factor_diagonal(): jax.scipy.linalg.solve_triangular(cholesky_factor, identity, lower=True)  40.9 us
    all_gather x2, blocking collectives, picked(): lax.all_gather(array, axis)  38.7 us
  transfers between devices with their start and end apart: 8, of which 8 were waited for; matrix products, arithmetic and copies ran while one was open for 1% of the time, Pallas kernels for 0%

commit v1 on v0

--- a/solution.py
+++ b/solution.py
@@ -14,7 +14,7 @@
 def from_root(array, axes, root):
     array = jnp.where(lax.axis_index(axes) == root, array, jnp.zeros_like(array))
     for axis in axes:
-        array = lax.psum(array, axis)
+        array = jnp.sum(lax.all_gather(array, axis), axis=0)
     return array
 
 

time: 725 us -> 629 us (0.87)
  waiting for transfers between devices: 523 us -> 417 us
  other arithmetic: 114 us -> 126 us
    psum x4 -> x0, waiting for transfers between devices: 385 us -> none  [from_root(): array = lax.psum(array, axis)]
    all_gather x0 -> x4, waiting for transfers between devices: none -> 280 us  [from_root(): array = jnp.sum(lax.all_gather(array, axis), axis=0)]
    reduce_sum x0 -> x4, other arithmetic: none -> 13.1 us  [from_root(): array = jnp.sum(lax.all_gather(array, axis), axis=0)]
where the time goes in v1:
time: 629 us; the launch traced here: 628 us
  waiting for transfers between devices  417 us (66%)
  other arithmetic  126 us (20%)
  blocking collectives  38.7 us (6%)
  between operations  17.1 us (3%)
  local copies, waits for them, and re-layouts  14.4 us (2%)
  matrix products  14.1 us (2%)
    all_gather x4, waiting for transfers between devices, from_root(): array = jnp.sum(lax.all_gather(array, axis), axis=0)  280 us
    all_gather x4, waiting for transfers between devices, picked(): lax.all_gather(array, axis)  137 us
    another operation x13, other arithmetic, factor_diagonal(): cholesky_factor = jnp.linalg.cholesky(diagonal)  68.5 us
    another operation x7, other arithmetic, factor_diagonal(): jax.scipy.linalg.solve_triangular(cholesky_factor, identity, lower=True)  40.9 us
    all_gather x2, blocking collectives, picked(): lax.all_gather(array, axis)  38.7 us
    reduce_sum x4, other arithmetic, from_root(): array = jnp.sum(lax.all_gather(array, axis), axis=0)  13.1 us
  transfers between devices with their start and end apart: 8, of which 8 were waited for; matrix products, arithmetic and copies ran while one was open for 1% of the time, Pallas kernels for 0%

profile of v1, /device:TPU:1, one launch (start us, length us, event | category | flops | bytes accessed | tf_op | source)
XLA Modules:
  0.0 628.1 jit_solution(13421157774469658679)
XLA Ops:
  7.2 1.9 broadcast_select_fusion.1
  9.2 112.5 %all-gather.21.cloned.1.call-done = f32[4096,512]{1,0:T(8,128)} async-done(((f32[256,512]{1,0:T(8,128)}), f32[4096,512]{1,0:T(8,128)}) %all-gather.21.cloned.1.call-update) | async-done | bytes 8388624 | tf_op jit(solution)/shard_map/all_gather | solution.py:17
  121.7 5.2 reduce_sum.36
  127.0 31.0 %all-gather.23.cloned.1.call-done = f32[512,512]{1,0:T(8,128)} async-done(((f32[256,512]{1,0:T(8,128)}), f32[512,512]{1,0:T(8,128)}) %all-gather.23.cloned.1.call-update) | async-done | bytes 1048592 | tf_op jit(solution)/shard_map/all_gather | solution.py:17
  159.6 11.7 %cholesky.130 = f32[128,128]{1,0:T(8,128)S(1)} custom-call(f32[128,128]{1,0:T(8,128)S(1)} %cholesky.194), custom_call_target="Cholesky" | custom-call | tf_op jit(solution)/shard_map/jit(cholesky)/cholesky | solution.py:26
  171.3 9.8 %custom-call.17 = f32[1,128,128]{1,2,0:T(8,128)S(1)} custom-call(f32[1,128,128]{2,1,0:T(8,128)S(1)} %get-tuple-element.58), custom_call_target="InvertDiagBlocksLowerTriangular" | custom-call | tf_op jit(solution)/shard_map/jit(cholesky)/cholesky | solution.py:26
  181.6 11.7 %cholesky.147 = f32[128,128]{1,0:T(8,128)S(1)} custom-call(f32[128,128]{1,0:T(8,128)S(1)} %convolution_subtract_fusion.5), custom_call_target="Cholesky" | custom-call | tf_op jit(solution)/shard_map/jit(cholesky)/cholesky | solution.py:26
  195.5 4.2 while.4
  196.3 1.4 bitcast_dynamic-update-slice_fusion.4
  198.3 1.4 bitcast_dynamic-update-slice_fusion.4
  199.7 19.7 %custom-call.18 = f32[2,128,128]{1,2,0:T(8,128)S(1)} custom-call(f32[2,128,128]{2,1,0:T(8,128)S(1)} %get-tuple-element.19), custom_call_target="InvertDiagBlocksLowerTriangular" | custom-call | tf_op jit(solution)/shard_map/jit(_solve_triangular)/triangular_solve | solution.py:29
  221.0 2.3 gather_fusion
  224.6 19.3 %all-gather.10 = f32[16,1,256]{2,1,0:T(1,128)S(1)} all-gather(f32[1,1,256]{2,1,0:T(1,128)S(1)} %bitcast.90), channel_id=5, replica_groups=mesh['prow_0'=16,'prow_1'=2,'pcol'=16] {'pcol'}, dimensions={0}, use_global_device_ids=true | all-gather | bytes 17408 | tf_op jit(solution)/shard_map/all_gather | solution.py:22
  244.0 22.0 %all-gather.27.cloned.1.call-done = f32[4096,256]{1,0:T(8,128)} async-done(((f32[256,256]{1,0:T(8,128)}), f32[4096,256]{1,0:T(8,128)}) %all-gather.27.cloned.1.call-update) | async-done | bytes 4194320 | tf_op jit(solution)/shard_map/all_gather | solution.py:22
  266.0 1.9 convolution_multiply_fusion.1
  267.9 45.0 %all-gather.25.cloned.1.call-done = f32[4096,256]{0,1:T(8,128)} async-done(((f32[256,256]{0,1:T(8,128)}), f32[4096,256]{0,1:T(8,128)}) %all-gather.25.cloned.1.call-update) | async-done | bytes 4194320 | tf_op jit(solution)/shard_map/all_gather | solution.py:22
  312.9 2.9 broadcast_select_fusion
  315.8 105.6 %all-gather.29.cloned.1.call-done = f32[4096,512]{1,0:T(8,128)} async-done(((f32[256,512]{1,0:T(8,128)}), f32[4096,512]{1,0:T(8,128)}) %all-gather.29.cloned.1.call-update) | async-done | bytes 8388624 | tf_op jit(solution)/shard_map/all_gather | solution.py:17
  421.5 5.2 reduce_sum.38
  427.0 30.8 %all-gather.31.cloned.1.call-done = f32[512,512]{1,0:T(8,128)} async-done(((f32[256,512]{1,0:T(8,128)}), f32[512,512]{1,0:T(8,128)}) %all-gather.31.cloned.1.call-update) | async-done | bytes 1048592 | tf_op jit(solution)/shard_map/all_gather | solution.py:17
  459.4 11.7 %cholesky.164 = f32[128,128]{1,0:T(8,128)S(1)} custom-call(f32[128,128]{1,0:T(8,128)S(1)} %cholesky.197), custom_call_target="Cholesky" | custom-call | tf_op jit(solution)/shard_map/jit(cholesky)/cholesky | solution.py:26
  471.8 9.8 %custom-call.19 = f32[1,128,128]{1,2,0:T(8,128)S(1)} custom-call(f32[1,128,128]{2,1,0:T(8,128)S(1)} %get-tuple-element.54), custom_call_target="InvertDiagBlocksLowerTriangular" | custom-call | tf_op jit(solution)/shard_map/jit(cholesky)/cholesky | solution.py:26
  482.1 11.7 %cholesky.181 = f32[128,128]{1,0:T(8,128)S(1)} custom-call(f32[128,128]{1,0:T(8,128)S(1)} %convolution_subtract_fusion.4), custom_call_target="Cholesky" | custom-call | tf_op jit(solution)/shard_map/jit(cholesky)/cholesky | solution.py:26
  495.8 2.6 gather_fusion.1
  498.5 4.0 while.5
  499.1 1.4 bitcast_dynamic-update-slice_fusion.5
  502.5 19.7 %custom-call.20 = f32[2,128,128]{1,2,0:T(8,128)S(1)} custom-call(f32[2,128,128]{2,1,0:T(8,128)S(1)} %get-tuple-element.20), custom_call_target="InvertDiagBlocksLowerTriangular" | custom-call | tf_op jit(solution)/shard_map/jit(_solve_triangular)/triangular_solve | solution.py:29
  525.2 19.3 %all-gather.11 = f32[16,1,256]{2,1,0:T(1,128)S(1)} all-gather(f32[1,1,256]{2,1,0:T(1,128)S(1)} %bitcast.89), channel_id=10, replica_groups=mesh['prow_0'=16,'prow_1'=2,'pcol'=16] {'pcol'}, dimensions={0}, use_global_device_ids=true | all-gather | bytes 17408 | tf_op jit(solution)/shard_map/all_gather | solution.py:22
  545.2 24.0 %all-gather.33.cloned.1.call-done = f32[4096,256]{1,0:T(8,128)} async-done(((f32[256,256]{1,0:T(8,128)}), f32[4096,256]{1,0:T(8,128)}) %all-gather.33.cloned.1.call-update) | async-done | bytes 4194320 | tf_op jit(solution)/shard_map/all_gather | solution.py:22
  570.8 46.1 %all-gather.35.cloned.1.call-done = f32[4096,256]{1,0:T(8,128)} async-done(((f32[256,256]{1,0:T(8,128)}), f32[4096,256]{1,0:T(8,128)}) %all-gather.35.cloned.1.call-update) | async-done | bytes 4194320 | tf_op jit(solution)/shard_map/all_gather | solution.py:22
  616.9 1.9 convolution_multiply_fusion
  618.9 2.4 fusion
  (84 shorter events, 18.6 us)
Async XLA Ops:
  7.2 114.5 %all-gather.21.cloned.1.call-start = ((), (), s32[]{:S(2)}) async-start(), calls=%async_computation | async-start | bytes 8912896 | tf_op jit(solution)/shard_map/all_gather | solution.py:17
  9.1 148.8 %all-gather.23.cloned.1.call-start = ((), (), s32[]{:S(2)}) async-start(), calls=%async_computation.1 | async-start | bytes 1572864 | tf_op jit(solution)/shard_map/all_gather | solution.py:17
  126.9 139.1 %all-gather.27.cloned.1.call-start = ((), (), s32[]{:S(2)}) async-start(), calls=%async_computation.3 | async-start | bytes 4456448 | tf_op jit(solution)/shard_map/all_gather | solution.py:22
  159.3 64.1 %copy-start = (f32[256,512]{1,0:T(8,128)S(1)}, f32[256,512]{1,0:T(8,128)}, u32[]{:S(2)}) copy-start(f32[256,512]{1,0:T(8,128)} %param.4) | copy-start | bytes 1572868
  221.0 91.9 %all-gather.25.cloned.1.call-start = ((), (), s32[]{:S(2)}) async-start(), calls=%async_computation.2 | async-start | bytes 4456448 | tf_op jit(solution)/shard_map/all_gather | solution.py:22
  224.5 196.9 %all-gather.29.cloned.1.call-start = ((), (), s32[]{:S(2)}) async-start(), calls=%async_computation.4 | async-start | bytes 8912896 | tf_op jit(solution)/shard_map/all_gather | solution.py:17
  315.8 142.0 %all-gather.31.cloned.1.call-start = ((), (), s32[]{:S(2)}) async-start(), calls=%async_computation.5 | async-start | bytes 1572864 | tf_op jit(solution)/shard_map/all_gather | solution.py:17
  426.7 142.5 %all-gather.33.cloned.1.call-start = ((), (), s32[]{:S(2)}) async-start(), calls=%async_computation.6 | async-start | bytes 4456448 | tf_op jit(solution)/shard_map/all_gather | solution.py:22
  459.3 65.7 %slice-start = ((f32[4096,256]{0,1:T(8,128)}), f32[256,256]{0,1:T(8,128)S(1)}, s32[]{:S(2)}) async-start(f32[4096,256]{0,1:T(8,128)} %all-gather.25.cloned.1.call-done), calls=%async_computation.8 | async-start | bytes 524288 | tf_op jit(solution)/shard_map/jit(dynamic_index_in_dim)/dynamic_slice | solution.py:22
  524.2 92.7 %all-gather.35.cloned.1.call-start = ((), (), s32[]{:S(2)}) async-start(), calls=%async_computation.7 | async-start | bytes 4456448 | tf_op jit(solution)/shard_map/all_gather | solution.py:22
Sparse Core Ops, SparseCore 0:
  10.6 110.9 all-gather.20
  127.0 30.9 all-gather.22
  221.1 44.8 all-gather.26
  267.9 44.9 all-gather.24
  315.9 105.5 all-gather.28
  426.8 30.9 all-gather.30
  524.3 44.7 all-gather.32
  571.9 44.9 all-gather.34
